TPU v7x, 128 devices: a whole 4x4x4 slice. The times are simulated.
128 devices in a mesh: row: 32 (over z, x, core), col: 4 (over y).
Axes of the slice: x: 4, y: 4, z: 4, core: 2. Of those that a mesh axis runs over, the one named last changes fastest.
Arguments:
- prior_scores: float32 [12288, 12288], P('row', 'col'), may hold values from 0.001 to 10
- tiles_first: bfloat16 [96, 5, 128, 128], P('row'), may hold values from 0 to 1, as said below
- columns_first: int32 [96, 5], P('row'), may hold values from 0 to 95, as said below
- tiles_second: bfloat16 [96, 5, 128, 128], P('col'), may hold values from 0 to 1, as said below
- columns_second: int32 [96, 5], P('col'), may hold values from 0 to 95, as said below
Outputs:
- alignment: float32 [12288, 12288], P('row', 'col')
Inputs may be any that keep to these rules, and one draw needn't show every extreme that they name: `tiles_first`: in every block row, the block in the first slot has entries of 0.5 or more on its diagonal. `tiles_second`: in every block row, the block in the first slot has entries of 0.5 or more on its diagonal. `columns_first`: each block row lists 5 different block columns. `columns_second`: each block row lists 5 different block columns.
All inputs are finite; a program needn't handle non-finite values.
Results may differ from a plain program's by a relative error of at most 0.0004.
The roundings to bfloat16 on the way count: a program that leaves them out, or rounds other values in their place, can miss the bound.
Values may be sent and summed in bfloat16 or wider, within the bound.
A program may use at most 192 MiB of HBM per device.

v0:
```python
import functools
import jax
import jax.numpy as jnp
from jax import lax
from jax.sharding import Mesh
from jax.sharding import PartitionSpec as P

ITERS = 2
ROW = ("row_0", "row_1", "row_2")
ROW_COL = ("row_0", "row_1", "row_2", "col")
mixing = 0.8


def by_axis(value, axes):
    return functools.reduce(lax.psum, axes, value)


def second_product(features, tile_set, columns, inverse):
    tile_size = tile_set.shape[2]
    blocks = features.reshape(-1, tile_size, features.shape[1])
    picked = jnp.take(blocks, columns, axis=0)
    result = jnp.einsum("jsoi,jsin->jon", tile_set, picked, preferred_element_type=jnp.float32)
    result = result.reshape(-1, features.shape[1]) * inverse[:, None]
    return result.astype(jnp.bfloat16)


def first_product(slab_data, tile_set, columns, inverse):
    tile_size = tile_set.shape[2]
    blocks = slab_data.reshape(slab_data.shape[0], -1, tile_size)
    picked = jnp.take(blocks, columns, axis=1)
    result = jnp.einsum("cisk,isok->cio", picked, tile_set, preferred_element_type=jnp.float32)
    result = result.reshape(slab_data.shape[0], -1) * inverse[None, :]
    return result.astype(jnp.bfloat16)


def local(prior_scores, tiles_first, columns_first, tiles_second, columns_second):
    prior_cols = prior_scores.T
    row_count = lax.axis_size(ROW)
    cell_count = float(
        prior_scores.shape[0] * row_count * prior_scores.shape[1] * lax.axis_size("col")
    )
    all_first, all_columns = (
        lax.all_gather(tiles_first, ROW, axis=0, tiled=True),
        lax.all_gather(columns_first, ROW, axis=0, tiled=True),
    )
    inverse_first = 1.0 / jnp.sum(all_first, axis=(1, 3), dtype=jnp.float32).reshape(-1)
    inverse_second = 1.0 / jnp.sum(tiles_second, axis=(1, 3), dtype=jnp.float32).reshape(-1)
    prior_sum = by_axis(jnp.sum(prior_cols), ROW_COL)
    current_state = prior_cols
    for iteration in range(ITERS):
        current = current_state.astype(jnp.bfloat16)
        gathered = lax.all_gather(current, "col", axis=0, tiled=True)
        mixed_cols = second_product(gathered, tiles_second, columns_second, inverse_second)
        slab_data = lax.all_to_all(mixed_cols, ROW, split_axis=0, concat_axis=1, tiled=True)
        propagated = first_product(slab_data, all_first, all_columns, inverse_first)
        partial_value = jnp.sum(propagated.astype(jnp.float32))
        returned = lax.all_to_all(propagated, ROW, split_axis=1, concat_axis=0, tiled=True)
        slab_sum = by_axis(partial_value, ROW_COL)
        grand_total = mixing * slab_sum + (1.0 - mixing) * prior_sum
        updated = mixing * returned.astype(jnp.float32) + (1.0 - mixing) * prior_cols
        current_state = updated / (grand_total / cell_count)
    return current_state.T


def solution(mesh):
    finer = Mesh(
        mesh.devices.reshape(4, 4, 2, mesh.shape["col"]), ("row_0", "row_1", "row_2", "col")
    )
    return jax.shard_map(
        local,
        mesh=finer,
        in_specs=(
            P(ROW, "col"),
            P(ROW, None, None, None),
            P(ROW, None),
            P("col", None, None, None),
            P("col", None),
        ),
        out_specs=P(ROW, "col"),
        check_vma=False,
    )
```

profile of v0, /device:TPU:0, one launch (start us, length us, event | category | flops | bytes accessed | tf_op | source)
XLA Modules:
  0.0 633.5 jit_solution(3991835615490677281)
XLA Ops:
  6.5 7.0 %fusion.31 = (f32[]{:T(128)}, bf16[3072,384]{0,1:T(8,128)(2,1)}) fusion(f32[384,3072]{1,0:T(8,128)} %param.9), kind=kLoop, calls=%fused_computation.54 | loop fusion | flops 2359295 | bytes 7077892 | tf_op jit(solution)/shard_map/reduce_sum | solution.py:48
  13.6 0.7 all-gather.7.cloned.1.call-update
  14.6 2.7 convert_reduce_fusion.1
  17.4 90.7 %all-gather.5.cloned.1.call-done = bf16[12288,384]{0,1:T(8,128)(2,1)} async-done(((bf16[3072,384]{0,1:T(8,128)(2,1)}), bf16[12288,384]{0,1:T(8,128)(2,1)}) %all-gather.5.cloned.1.call-update) | async-done | bytes 9437200 | tf_op jit(solution)/shard_map/all_gather | solution.py:52
  108.1 12.6 %copy.59 = bf16[12288,384]{1,0:T(8,128)(2,1)} copy(bf16[12288,384]{0,1:T(8,128)(2,1)} %all-gather.5.cloned.1.call-done) | data formatting | bytes 18874368 | tf_op jit(solution)/shard_map/all_gather | solution.py:52
  120.7 12.7 %gather_fusion = bf16[120,128,384]{2,1,0:T(8,128)(2,1)} fusion(bf16[96,128,384]{2,1,0:T(8,128)(2,1)} %bitcast.69, s32[1024]{0:T(1024)S(1)} %pad_clamp_fusion.1), kind=kCustom, calls=%fused_computation.clone | custom fusion | bytes 23593440 | tf_op jit(solution)/shard_map/jit(_take)/gather | solution.py:21
  133.4 8.3 %fusion.8 = f32[24,384,128,1]{1,2,3,0:T(8,128)S(1)} fusion(bf16[24,5,128,128]{3,2,1,0:T(8,128)(2,1)} %param.12, bf16[24,5,128,384]{3,2,1,0:T(8,128)(2,1)} %bitcast.75, pred[24,5]{1,0:T(8,128)(4,1)S(1)} %copy.56), kind=kOutput, calls=%fused_computation.13 | convolution fusion | flops 1515847680 | bytes 20447352 | tf_op jit(solution)/shard_map/jsoi,jsin->jon/dot_general | solution.py:22
  141.7 1.9 multiply_convert_fusion.5
  143.6 7.2 %all-to-all-start = ((bf16[32,96,384]{2,1,0:T(8,128)(2,1)}), bf16[32,96,384]{2,1,0:T(8,128)(2,1)S(1)}, u32[]{:S(2)}, u32[]{:S(2)}) async-start(bf16[32,96,384]{2,1,0:T(8,128)(2,1)} %multiply_convert_fusion.5), calls=%async_computation | async-start | bytes 4718592 | tf_op jit(solution)/shard_map/all_to_all | solution.py:54
  150.9 70.6 %all-gather = s32[32,3,5]{2,1,0:T(4,128)S(1)} all-gather(s32[1,3,5]{2,1,0:T(4,128)S(1)} %bitcast.80), channel_id=1, replica_groups=mesh['row_0'=4,'row_1'=4,'row_2'=2,'col'=4] {'row_0','row_1','row_2'}, dimensions={0}, use_global_device_ids=true | all-gather | bytes 1980 | tf_op jit(solution)/shard_map/all_gather | solution.py:44
  222.0 2.2 copy.61
  224.3 5.1 reshape.106
  229.4 2.6 copy.63
  232.0 14.9 %gather_fusion.1 = bf16[480,96,128]{2,1,0:T(8,128)(2,1)} fusion(bf16[96,96,128]{2,0,1:T(8,128)(2,1)S(1)} %copy.63, s32[1024]{0:T(1024)S(1)} %pad_clamp_fusion), kind=kCustom, calls=%fused_computation.1.clone | custom fusion | bytes 23594880 | tf_op jit(solution)/shard_map/jit(_take)/gather | solution.py:30
  246.8 6.6 %convert_reduce_fusion = f32[96,128]{1,0:T(8,128)S(1)} fusion(bf16[96,5,128,128]{3,2,1,0:T(8,128)(2,1)} %all-gather.7.cloned.1.call-done), kind=kLoop, calls=%fused_computation.4 | loop fusion | flops 15716352 | bytes 15777792 | tf_op jit(solution)/shard_map/reduce_sum | solution.py:46
  253.5 14.1 %convert_reduce_fusion.3 = (f32[]{:T(128)}, f32[96,96,128]{2,0,1:T(8,128)}) fusion(f32[96,128]{1,0:T(8,128)S(1)} %broadcast_divide_fusion, bf16[96,5,128,128]{3,2,1,0:T(8,128)(2,1)} %all-gather.7.cloned.1.call-done, bf16[96,5,96,128]{3,2,1,0:T(8,128)(2,1)} %bitcast.70, pred[96,5]{1,0:T(8,128)(4,1)S(1)} %copy.55), kind=kOutput, calls=%fused_computation.34 | convolution fusion | flops 1520566272 | bytes 32293348 | tf_op jit(solution)/shard_map/cisk,isok->cio/dot_general | solution.py:31
  267.6 7.2 %copy.64 = f32[96,96,128]{2,1,0:T(8,128)} copy(f32[96,96,128]{2,0,1:T(8,128)} %get-tuple-element.18) | data formatting | bytes 9437184 | tf_op jit(solution)/shard_map/cisk,isok->cio/transpose | solution.py:31
  274.8 6.3 reshape.107
  281.0 2.9 multiply_convert_fusion.4
  283.9 2.2 copy.65
  286.1 5.2 all-to-all-start.1
  291.4 6.0 copy.66
  297.5 25.0 %all-reduce.2 = (f32[]{:T(128)}, f32[]{:T(128)}) all-reduce(f32[]{:T(128)} %get-tuple-element.17, f32[]{:T(128)} %get-tuple-element.15), channel_id=1, replica_groups=mesh['row_0'=4,'row_1'=4,'row_2'=2,'col'=4] {'row_0'}, use_global_device_ids=true, to_apply=%region_3.6 | all-reduce | flops 2 | bytes 16 | tf_op jit(solution)/shard_map/psum | solution.py:15
  322.5 11.8 %all-reduce.1 = (f32[]{:T(128)}, f32[]{:T(128)}) all-reduce(f32[]{:T(128)} %get-tuple-element.11, f32[]{:T(128)} %get-tuple-element.12), channel_id=1, replica_groups=mesh['row_0'=4,'row_1'=4,'row_2'=2,'col'=4] {'row_1'}, use_global_device_ids=true, to_apply=%region_4.7 | all-reduce | flops 2 | bytes 16 | tf_op jit(solution)/shard_map/psum | solution.py:15
  334.2 3.1 all-reduce.3
  337.4 11.1 %all-reduce = (f32[]{:T(128)}, f32[]{:T(128)}) all-reduce(f32[]{:T(128)} %get-tuple-element.13, f32[]{:T(128)} %get-tuple-element.14), channel_id=1, replica_groups=mesh['row_0'=4,'row_1'=4,'row_2'=2,'col'=4] {'col'}, use_global_device_ids=true, to_apply=%region_6.9 | all-reduce | flops 2 | bytes 16 | tf_op jit(solution)/shard_map/psum | solution.py:15
  350.4 1.7 copy-done
  352.1 2.1 fusion.20
  354.2 86.6 %all-gather.9.cloned.1.call-done = bf16[12288,384]{1,0:T(8,128)(2,1)} async-done(((bf16[3072,384]{1,0:T(8,128)(2,1)}), bf16[12288,384]{1,0:T(8,128)(2,1)}) %all-gather.9.cloned.1.call-update) | async-done | bytes 9437200 | tf_op jit(solution)/shard_map/all_gather | solution.py:52
  440.8 12.3 %gather_fusion.2 = bf16[120,128,384]{2,1,0:T(8,128)(2,1)} fusion(bf16[96,128,384]{2,1,0:T(8,128)(2,1)} %bitcast.73, s32[1024]{0:T(1024)S(1)} %pad_clamp_fusion.1), kind=kCustom, calls=%fused_computation.2.clone | custom fusion | bytes 23593440 | tf_op jit(solution)/shard_map/jit(_take)/gather | solution.py:21
  453.1 8.2 %fusion.5 = f32[24,384,128,1]{1,2,3,0:T(8,128)S(1)} fusion(bf16[24,5,128,128]{3,2,1,0:T(8,128)(2,1)} %param.12, bf16[24,5,128,384]{3,2,1,0:T(8,128)(2,1)} %bitcast.74, pred[24,5]{1,0:T(8,128)(4,1)S(1)} %copy.56), kind=kOutput, calls=%fused_computation.10 | convolution fusion | flops 1515847680 | bytes 20447352 | tf_op jit(solution)/shard_map/jsoi,jsin->jon/dot_general | solution.py:22
  461.9 38.7 %all_to_all.46 = bf16[32,96,384]{2,1,0:T(8,128)(2,1)S(1)} all-to-all(bf16[32,96,384]{2,1,0:T(8,128)(2,1)S(1)} %multiply_convert_fusion.2), channel_id=1, replica_groups=mesh['row_0'=4,'row_1'=4,'row_2'=2,'col'=4] {'row_0','row_1','row_2'}, dimensions={0} | all-to-all | bytes 4718592 | tf_op jit(solution)/shard_map/all_to_all | solution.py:54
  500.6 0.9 copy.68
  501.4 2.5 reshape.110
  503.9 2.6 copy.70
  506.5 14.9 %gather_fusion.3 = bf16[480,96,128]{2,1,0:T(8,128)(2,1)} fusion(bf16[96,96,128]{2,0,1:T(8,128)(2,1)S(1)} %copy.70, s32[1024]{0:T(1024)S(1)} %pad_clamp_fusion), kind=kCustom, calls=%fused_computation.3.clone | custom fusion | bytes 23594880 | tf_op jit(solution)/shard_map/jit(_take)/gather | solution.py:30
  521.4 14.1 %convert_reduce_fusion.2 = (f32[]{:T(128)}, f32[96,96,128]{2,0,1:T(8,128)}) fusion(f32[96,128]{1,0:T(8,128)S(1)} %broadcast_divide_fusion, bf16[96,5,128,128]{3,2,1,0:T(8,128)(2,1)} %all-gather.7.cloned.1.call-done, bf16[96,5,96,128]{3,2,1,0:T(8,128)(2,1)} %bitcast.71, pred[96,5]{1,0:T(8,128)(4,1)S(1)} %copy.55), kind=kOutput, calls=%fused_computation.29 | convolution fusion | flops 1520566272 | bytes 32293348 | tf_op jit(solution)/shard_map/cisk,isok->cio/dot_general | solution.py:31
  535.5 7.2 %copy.71 = f32[96,96,128]{2,1,0:T(8,128)} copy(f32[96,96,128]{2,0,1:T(8,128)} %get-tuple-element.20) | data formatting | bytes 9437184 | tf_op jit(solution)/shard_map/cisk,isok->cio/transpose | solution.py:31
  542.7 6.1 reshape.111
  548.8 2.9 multiply_convert_fusion.1
  551.7 2.2 copy.72
  554.0 4.1 all-to-all-start.3
  558.1 31.0 %psum.92 = f32[]{:T(128)} all-reduce(f32[]{:T(128)} %get-tuple-element.19), channel_id=1, replica_groups=mesh['row_0'=4,'row_1'=4,'row_2'=2,'col'=4] {'row_0'}, use_global_device_ids=true, to_apply=%region_13.16 | all-reduce | flops 1 | bytes 8 | tf_op jit(solution)/shard_map/psum | solution.py:15
  589.1 11.7 %psum.93 = f32[]{:T(128)} all-reduce(f32[]{:T(128)} %psum.92), channel_id=1, replica_groups=mesh['row_0'=4,'row_1'=4,'row_2'=2,'col'=4] {'row_1'}, use_global_device_ids=true, to_apply=%region_14.17 | all-reduce | flops 1 | bytes 8 | tf_op jit(solution)/shard_map/psum | solution.py:15
  600.8 3.1 psum.94
  603.9 10.1 %psum.95 = f32[]{:T(128)} all-reduce(f32[]{:T(128)} %psum.94), channel_id=1, replica_groups=mesh['row_0'=4,'row_1'=4,'row_2'=2,'col'=4] {'col'}, use_global_device_ids=true, to_apply=%region_16.19 | all-reduce | flops 1 | bytes 8 | tf_op jit(solution)/shard_map/psum | solution.py:15
  615.2 5.5 fusion.18
  620.7 6.0 copy.73
  (35 shorter events, 2.8 us)
Async XLA Ops:
  6.5 7.8 %copy-start.1 = (s32[24,5]{0,1:T(8,128)S(1)}, s32[24,5]{0,1:T(8,128)}, u32[]{:S(2)}) copy-start(s32[24,5]{0,1:T(8,128)} %param.13) | copy-start | bytes 1444
  6.5 101.6 %all-gather.5.cloned.1.call-start = ((), (), s32[]{:S(2)}) async-start(), calls=%async_computation.4 | async-start | bytes 11796480 | tf_op jit(solution)/shard_map/all_gather | solution.py:52
  13.5 233.3 %all-gather.7.cloned.1.call-start = ((), (), s32[]{:S(2)}) async-start(), calls=%async_computation.5 | async-start | bytes 16220160 | tf_op jit(solution)/shard_map/all_gather | solution.py:43
  141.7 9.1 %copy-start.2 = (s32[3,5]{1,0:T(4,128)S(1)}, s32[3,5]{1,0:T(4,128)}, u32[]{:S(2)}) copy-start(s32[3,5]{1,0:T(4,128)} %param.11) | copy-start | bytes 184
  143.6 78.4 %all-to-all-start = ((bf16[32,96,384]{2,1,0:T(8,128)(2,1)}), bf16[32,96,384]{2,1,0:T(8,128)(2,1)S(1)}, u32[]{:S(2)}, u32[]{:S(2)}) async-start(bf16[32,96,384]{2,1,0:T(8,128)(2,1)} %multiply_convert_fusion.5), calls=%async_computation | async-start | bytes 4718592 | tf_op jit(solution)/shard_map/all_to_all | solution.py:54
  286.1 63.6 %all-to-all-start.1 = ((bf16[96,32,384]{2,0,1:T(8,128)(2,1)}), bf16[96,32,384]{2,0,1:T(8,128)(2,1)S(1)}, u32[]{:S(2)}, u32[]{:S(2)}) async-start(bf16[96,32,384]{2,0,1:T(8,128)(2,1)} %copy.65), calls=%async_computation.1 | async-start | bytes 4718592 | tf_op jit(solution)/shard_map/all_to_all | solution.py:57
  291.4 149.4 %all-gather.9.cloned.1.call-start = ((), (), s32[]{:S(2)}) async-start(), calls=%async_computation.6 | async-start | bytes 11796480 | tf_op jit(solution)/shard_map/all_gather | solution.py:52
  349.8 2.3 copy-start
  554.0 60.5 %all-to-all-start.3 = ((bf16[96,32,384]{2,0,1:T(8,128)(2,1)}), bf16[96,32,384]{2,0,1:T(8,128)(2,1)S(1)}, u32[]{:S(2)}, u32[]{:S(2)}) async-start(bf16[96,32,384]{2,0,1:T(8,128)(2,1)} %copy.72), calls=%async_computation.3 | async-start | bytes 4718592 | tf_op jit(solution)/shard_map/all_to_all | solution.py:57
Sparse Core Ops, SparseCore 0:
  13.7 94.4 all-gather.4
  110.4 95.9 all-gather.6
  354.3 86.4 all-gather.8
where the time goes:
time: 642 us; the launch traced here: 633 us
  blocking collectives  216 us (34%)
  waiting for transfers between devices  178 us (28%)
  local copies, waits for them, and re-layouts  129 us (20%)
  matrix products  44.8 us (7%)
  other arithmetic  33.4 us (5%)
  starting transfers between devices  16.6 us (3%)
  between operations  15.3 us (2%)
    all_gather x2, waiting for transfers between devices, local(): gathered = lax.all_gather(current, 'col', axis=0, tiled=True)  177 us
    psum x8, blocking collectives, by_axis(): return functools.reduce(lax.psum, axes, value)  107 us
    all_gather x1, blocking collectives, local(): lax.all_gather(columns_first, ROW, axis=0, tiled=True)  70.6 us
    all_to_all x1, blocking collectives, local(): lax.all_to_all(mixed_cols, ROW, split_axis=0, concat_axis=1, tiled=True)  38.7 us
    gather x2, local copies, waits for them, and re-layouts, first_product(): picked = jnp.take(blocks, columns, axis=1)  29.8 us
    dot_general x2, matrix products, first_product(): jnp.einsum('cisk,isok->cio', picked, tile_set, preferred_element_type=jnp...  28.2 us
    gather x2, local copies, waits for them, and re-layouts, second_product(): picked = jnp.take(blocks, columns, axis=0)  25 us
    dot_general x2, matrix products, second_product(): jnp.einsum('jsoi,jsin->jon', tile_set, picked, preferred_element_type=jnp...  16.5 us
  transfers between devices with their start and end apart: 6, of which 2 were waited for; matrix products, arithmetic and copies ran while one was open for 11% of the time, Pallas kernels for 0%

commit v1 on v0

--- a/solution.py
+++ b/solution.py
@@ -51,7 +51,10 @@
         current = current_state.astype(jnp.bfloat16)
         gathered = lax.all_gather(current, "col", axis=0, tiled=True)
         mixed_cols = second_product(gathered, tiles_second, columns_second, inverse_second)
-        slab_data = lax.all_to_all(mixed_cols, ROW, split_axis=0, concat_axis=1, tiled=True)
+        slab_data = jnp.concatenate(
+            lax.all_to_all(jnp.stack(jnp.split(mixed_cols, lax.axis_size(ROW), axis=0)), ROW, 0, 0),
+            axis=1,
+        )
         propagated = first_product(slab_data, all_first, all_columns, inverse_first)
         partial_value = jnp.sum(propagated.astype(jnp.float32))
         returned = lax.all_to_all(propagated, ROW, split_axis=1, concat_axis=0, tiled=True)

time: 642 us -> 643 us (level)
  local copies, waits for them, and re-layouts: 129 us -> 150 us
  blocking collectives: 216 us -> 197 us
    unnamed x9 -> x71, local copies, waits for them, and re-layouts: 7.85 us -> 28.2 us
    all_gather x1, blocking collectives: 70.6 us -> 51.6 us  [local(): lax.all_gather(columns_first, ROW, axis=0, tiled=True)]
    another operation x0 -> x6, local copies, waits for them, and re-layouts: none -> 13.4 us  [the longest x4 12.8 us: first_product(): blocks = slab_data.reshape(slab_data.shape[0], -1, tile_size)]
    reshape x4 -> x2, local copies, waits for them, and re-layouts: 12.8 us -> 3.1 us  [local(): jnp.concatenate(lax.all_to_all(jnp.stack(jnp.split(mixed_cols, lax.axis_s...]
  transfers between devices with their start and end apart: 6 -> 6, of which waited for: 2 -> 2; matrix products, arithmetic and copies ran while one was open for 11% -> 14% of each run, Pallas kernels for 0% -> 0%
where the time goes in v1:
time: 643 us; the launch traced here: 634 us
  blocking collectives  197 us (31%)
  waiting for transfers between devices  178 us (28%)
  local copies, waits for them, and re-layouts  150 us (23%)
  matrix products  44.8 us (7%)
  other arithmetic  32 us (5%)
  starting transfers between devices  16.8 us (3%)
  between operations  15.5 us (2%)
    all_gather x2, waiting for transfers between devices, local(): gathered = lax.all_gather(current, 'col', axis=0, tiled=True)  177 us
    psum x8, blocking collectives, by_axis(): return functools.reduce(lax.psum, axes, value)  107 us
    all_gather x1, blocking collectives, local(): lax.all_gather(columns_first, ROW, axis=0, tiled=True)  51.6 us
    all_to_all x1, blocking collectives, local(): lax.all_to_all(jnp.stack(jnp.split(mixed_cols, lax.axis_size(ROW), axis=0...  38.7 us
    gather x2, local copies, waits for them, and re-layouts, first_product(): picked = jnp.take(blocks, columns, axis=1)  29.8 us
    dot_general x2, matrix products, first_product(): jnp.einsum('cisk,isok->cio', picked, tile_set, preferred_element_type=jnp...  28.2 us
    unnamed x71, local copies, waits for them, and re-layouts  28.2 us
    gather x2, local copies, waits for them, and re-layouts, second_product(): picked = jnp.take(blocks, columns, axis=0)  25 us
  transfers between devices with their start and end apart: 6, of which 2 were waited for; matrix products, arithmetic and copies ran while one was open for 14% of the time, Pallas kernels for 0%

profile of v1, /device:TPU:0, one launch (start us, length us, event | category | flops | bytes accessed | tf_op | source)
XLA Modules:
  0.0 634.5 jit_solution(3374534732944684079)
XLA Ops:
  6.5 7.0 %fusion.33 = (f32[]{:T(128)}, bf16[3072,384]{0,1:T(8,128)(2,1)}) fusion(f32[384,3072]{1,0:T(8,128)} %param.9), kind=kLoop, calls=%fused_computation.184 | loop fusion | flops 2359295 | bytes 7077892 | tf_op jit(solution)/shard_map/reduce_sum | solution.py:48
  13.6 0.7 all-gather.7.cloned.1.call-update
  14.6 2.7 convert_reduce_fusion.1
  17.3 90.8 %all-gather.5.cloned.1.call-done = bf16[12288,384]{0,1:T(8,128)(2,1)} async-done(((bf16[3072,384]{0,1:T(8,128)(2,1)}), bf16[12288,384]{0,1:T(8,128)(2,1)}) %all-gather.5.cloned.1.call-update) | async-done | bytes 9437200 | tf_op jit(solution)/shard_map/all_gather | solution.py:52
  108.1 12.6 %copy.88 = bf16[12288,384]{1,0:T(8,128)(2,1)} copy(bf16[12288,384]{0,1:T(8,128)(2,1)} %all-gather.5.cloned.1.call-done) | data formatting | bytes 18874368 | tf_op jit(solution)/shard_map/all_gather | solution.py:52
  120.7 12.7 %gather_fusion = bf16[120,128,384]{2,1,0:T(8,128)(2,1)} fusion(bf16[96,128,384]{2,1,0:T(8,128)(2,1)} %bitcast.333, s32[1024]{0:T(1024)S(1)} %pad_clamp_fusion.1), kind=kCustom, calls=%fused_computation.clone | custom fusion | bytes 23593440 | tf_op jit(solution)/shard_map/jit(_take)/gather | solution.py:21
  133.4 8.3 %fusion.8 = f32[24,384,128,1]{1,2,3,0:T(8,128)S(1)} fusion(bf16[24,5,128,128]{3,2,1,0:T(8,128)(2,1)} %param.12, bf16[24,5,128,384]{3,2,1,0:T(8,128)(2,1)} %bitcast.339, pred[24,5]{1,0:T(8,128)(4,1)S(1)} %copy.85), kind=kOutput, calls=%fused_computation.13 | convolution fusion | flops 1515847680 | bytes 20447352 | tf_op jit(solution)/shard_map/jsoi,jsin->jon/dot_general | solution.py:22
  142.2 0.6 constant_dynamic-update-slice_fusion.31
  162.7 7.4 %all-to-all-start = ((bf16[32,96,384]{2,1,0:T(8,128)(2,1)}), bf16[32,96,384]{2,1,0:T(8,128)(2,1)S(1)}, u32[]{:S(2)}, u32[]{:S(2)}) async-start(bf16[32,96,384]{2,1,0:T(8,128)(2,1)} %constant_dynamic-update-slice_fusion), calls=%async_computation | async-start | bytes 4718592 | tf_op jit(solution)/shard_map/all_to_all | solution.py:55
  170.1 51.6 %all-gather = s32[32,3,5]{2,1,0:T(4,128)S(1)} all-gather(s32[1,3,5]{2,1,0:T(4,128)S(1)} %bitcast.342), channel_id=1, replica_groups=mesh['row_0'=4,'row_1'=4,'row_2'=2,'col'=4] {'row_0','row_1','row_2'}, dimensions={0}, use_global_device_ids=true | all-gather | bytes 1980 | tf_op jit(solution)/shard_map/all_gather | solution.py:44
  222.3 2.2 copy.90
  224.5 5.1 reshape_reshape.6
  229.6 2.6 copy.92
  232.2 14.9 %gather_fusion.1 = bf16[480,96,128]{2,1,0:T(8,128)(2,1)} fusion(bf16[96,96,128]{2,0,1:T(8,128)(2,1)S(1)} %copy.92, s32[1024]{0:T(1024)S(1)} %pad_clamp_fusion), kind=kCustom, calls=%fused_computation.1.clone | custom fusion | bytes 23594880 | tf_op jit(solution)/shard_map/jit(_take)/gather | solution.py:30
  247.1 6.6 %convert_reduce_fusion = f32[96,128]{1,0:T(8,128)S(1)} fusion(bf16[96,5,128,128]{3,2,1,0:T(8,128)(2,1)} %all-gather.7.cloned.1.call-done), kind=kLoop, calls=%fused_computation.4 | loop fusion | flops 15716352 | bytes 15777792 | tf_op jit(solution)/shard_map/reduce_sum | solution.py:46
  253.8 14.1 %convert_reduce_fusion.3 = (f32[]{:T(128)}, f32[96,96,128]{2,0,1:T(8,128)}) fusion(f32[96,128]{1,0:T(8,128)S(1)} %broadcast_divide_fusion, bf16[96,5,128,128]{3,2,1,0:T(8,128)(2,1)} %all-gather.7.cloned.1.call-done, bf16[96,5,96,128]{3,2,1,0:T(8,128)(2,1)} %bitcast.334, pred[96,5]{1,0:T(8,128)(4,1)S(1)} %copy.84), kind=kOutput, calls=%fused_computation.37 | convolution fusion | flops 1520566272 | bytes 32293348 | tf_op jit(solution)/shard_map/cisk,isok->cio/dot_general | solution.py:31
  267.8 7.2 %copy.93 = f32[96,96,128]{2,1,0:T(8,128)} copy(f32[96,96,128]{2,0,1:T(8,128)} %get-tuple-element.18) | data formatting | bytes 9437184 | tf_op jit(solution)/shard_map/cisk,isok->cio/transpose | solution.py:31
  275.0 6.3 reshape.87
  281.3 2.9 multiply_convert_fusion.3
  284.2 2.2 copy.94
  286.4 5.3 all-to-all-start.1
  291.8 6.0 copy.95
  297.8 25.0 %all-reduce.2 = (f32[]{:T(128)}, f32[]{:T(128)}) all-reduce(f32[]{:T(128)} %get-tuple-element.17, f32[]{:T(128)} %get-tuple-element.15), channel_id=1, replica_groups=mesh['row_0'=4,'row_1'=4,'row_2'=2,'col'=4] {'row_0'}, use_global_device_ids=true, to_apply=%region_3.6 | all-reduce | flops 2 | bytes 16 | tf_op jit(solution)/shard_map/psum | solution.py:15
  322.8 11.8 %all-reduce.1 = (f32[]{:T(128)}, f32[]{:T(128)}) all-reduce(f32[]{:T(128)} %get-tuple-element.11, f32[]{:T(128)} %get-tuple-element.12), channel_id=1, replica_groups=mesh['row_0'=4,'row_1'=4,'row_2'=2,'col'=4] {'row_1'}, use_global_device_ids=true, to_apply=%region_4.7 | all-reduce | flops 2 | bytes 16 | tf_op jit(solution)/shard_map/psum | solution.py:15
  334.6 3.1 all-reduce.3
  337.7 11.1 %all-reduce = (f32[]{:T(128)}, f32[]{:T(128)}) all-reduce(f32[]{:T(128)} %get-tuple-element.13, f32[]{:T(128)} %get-tuple-element.14), channel_id=1, replica_groups=mesh['row_0'=4,'row_1'=4,'row_2'=2,'col'=4] {'col'}, use_global_device_ids=true, to_apply=%region_6.9 | all-reduce | flops 2 | bytes 16 | tf_op jit(solution)/shard_map/psum | solution.py:15
  350.8 1.7 copy-done
  352.5 2.1 fusion.21
  354.5 86.6 %all-gather.9.cloned.1.call-done = bf16[12288,384]{1,0:T(8,128)(2,1)} async-done(((bf16[3072,384]{1,0:T(8,128)(2,1)}), bf16[12288,384]{1,0:T(8,128)(2,1)}) %all-gather.9.cloned.1.call-update) | async-done | bytes 9437200 | tf_op jit(solution)/shard_map/all_gather | solution.py:52
  441.1 12.3 %gather_fusion.2 = bf16[120,128,384]{2,1,0:T(8,128)(2,1)} fusion(bf16[96,128,384]{2,1,0:T(8,128)(2,1)} %bitcast.337, s32[1024]{0:T(1024)S(1)} %pad_clamp_fusion.1), kind=kCustom, calls=%fused_computation.2.clone | custom fusion | bytes 23593440 | tf_op jit(solution)/shard_map/jit(_take)/gather | solution.py:21
  453.5 8.2 %fusion.5 = f32[24,384,128,1]{1,2,3,0:T(8,128)S(1)} fusion(bf16[24,5,128,128]{3,2,1,0:T(8,128)(2,1)} %param.12, bf16[24,5,128,384]{3,2,1,0:T(8,128)(2,1)} %bitcast.338, pred[24,5]{1,0:T(8,128)(4,1)S(1)} %copy.85), kind=kOutput, calls=%fused_computation.10 | convolution fusion | flops 1515847680 | bytes 20447352 | tf_op jit(solution)/shard_map/jsoi,jsin->jon/dot_general | solution.py:22
  462.9 38.7 %all_to_all.30 = bf16[32,96,384]{2,1,0:T(8,128)(2,1)S(1)} all-to-all(bf16[32,96,384]{2,1,0:T(8,128)(2,1)S(1)} %constant_dynamic-update-slice_fusion.32), channel_id=1, replica_groups=mesh['row_0'=4,'row_1'=4,'row_2'=2,'col'=4] {'row_0','row_1','row_2'}, dimensions={0} | all-to-all | bytes 4718592 | tf_op jit(solution)/shard_map/all_to_all | solution.py:55
  501.6 0.9 copy.97
  502.5 2.5 reshape_reshape.7
  505.0 2.6 copy.99
  507.5 14.9 %gather_fusion.3 = bf16[480,96,128]{2,1,0:T(8,128)(2,1)} fusion(bf16[96,96,128]{2,0,1:T(8,128)(2,1)S(1)} %copy.99, s32[1024]{0:T(1024)S(1)} %pad_clamp_fusion), kind=kCustom, calls=%fused_computation.3.clone | custom fusion | bytes 23594880 | tf_op jit(solution)/shard_map/jit(_take)/gather | solution.py:30
  522.4 14.1 %convert_reduce_fusion.2 = (f32[]{:T(128)}, f32[96,96,128]{2,0,1:T(8,128)}) fusion(f32[96,128]{1,0:T(8,128)S(1)} %broadcast_divide_fusion, bf16[96,5,128,128]{3,2,1,0:T(8,128)(2,1)} %all-gather.7.cloned.1.call-done, bf16[96,5,96,128]{3,2,1,0:T(8,128)(2,1)} %bitcast.335, pred[96,5]{1,0:T(8,128)(4,1)S(1)} %copy.84), kind=kOutput, calls=%fused_computation.33 | convolution fusion | flops 1520566272 | bytes 32293348 | tf_op jit(solution)/shard_map/cisk,isok->cio/dot_general | solution.py:31
  536.6 7.2 %copy.100 = f32[96,96,128]{2,1,0:T(8,128)} copy(f32[96,96,128]{2,0,1:T(8,128)} %get-tuple-element.20) | data formatting | bytes 9437184 | tf_op jit(solution)/shard_map/cisk,isok->cio/transpose | solution.py:31
  543.7 6.1 reshape.91
  549.9 2.9 multiply_convert_fusion.1
  552.8 2.2 copy.101
  555.0 4.1 all-to-all-start.3
  559.1 31.0 %psum.92 = f32[]{:T(128)} all-reduce(f32[]{:T(128)} %get-tuple-element.19), channel_id=1, replica_groups=mesh['row_0'=4,'row_1'=4,'row_2'=2,'col'=4] {'row_0'}, use_global_device_ids=true, to_apply=%region_13.16 | all-reduce | flops 1 | bytes 8 | tf_op jit(solution)/shard_map/psum | solution.py:15
  590.1 11.7 %psum.93 = f32[]{:T(128)} all-reduce(f32[]{:T(128)} %psum.92), channel_id=1, replica_groups=mesh['row_0'=4,'row_1'=4,'row_2'=2,'col'=4] {'row_1'}, use_global_device_ids=true, to_apply=%region_14.17 | all-reduce | flops 1 | bytes 8 | tf_op jit(solution)/shard_map/psum | solution.py:15
  601.8 3.1 psum.94
  604.9 10.1 %psum.95 = f32[]{:T(128)} all-reduce(f32[]{:T(128)} %psum.94), channel_id=1, replica_groups=mesh['row_0'=4,'row_1'=4,'row_2'=2,'col'=4] {'col'}, use_global_device_ids=true, to_apply=%region_16.19 | all-reduce | flops 1 | bytes 8 | tf_op jit(solution)/shard_map/psum | solution.py:15
  616.2 5.5 fusion.18
  621.7 6.0 copy.102
  (98 shorter events, 23.6 us)
Async XLA Ops:
  6.5 101.6 %all-gather.5.cloned.1.call-start = ((), (), s32[]{:S(2)}) async-start(), calls=%async_computation.4 | async-start | bytes 11796480 | tf_op jit(solution)/shard_map/all_gather | solution.py:52
  13.5 0.8 copy-start.1
  13.5 233.6 %all-gather.7.cloned.1.call-start = ((), (), s32[]{:S(2)}) async-start(), calls=%async_computation.5 | async-start | bytes 16220160 | tf_op jit(solution)/shard_map/all_gather | solution.py:43
  162.7 7.4 %copy-start.2 = (s32[3,5]{1,0:T(4,128)S(1)}, s32[3,5]{1,0:T(4,128)}, u32[]{:S(2)}) copy-start(s32[3,5]{1,0:T(4,128)} %param.11) | copy-start | bytes 184
  162.7 59.6 %all-to-all-start = ((bf16[32,96,384]{2,1,0:T(8,128)(2,1)}), bf16[32,96,384]{2,1,0:T(8,128)(2,1)S(1)}, u32[]{:S(2)}, u32[]{:S(2)}) async-start(bf16[32,96,384]{2,1,0:T(8,128)(2,1)} %constant_dynamic-update-slice_fusion), calls=%async_computation | async-start | bytes 4718592 | tf_op jit(solution)/shard_map/all_to_all | solution.py:55
  286.4 63.7 %all-to-all-start.1 = ((bf16[96,32,384]{2,0,1:T(8,128)(2,1)}), bf16[96,32,384]{2,0,1:T(8,128)(2,1)S(1)}, u32[]{:S(2)}, u32[]{:S(2)}) async-start(bf16[96,32,384]{2,0,1:T(8,128)(2,1)} %copy.94), calls=%async_computation.1 | async-start | bytes 4718592 | tf_op jit(solution)/shard_map/all_to_all | solution.py:60
  291.7 149.4 %all-gather.9.cloned.1.call-start = ((), (), s32[]{:S(2)}) async-start(), calls=%async_computation.6 | async-start | bytes 11796480 | tf_op jit(solution)/shard_map/all_gather | solution.py:52
  350.1 2.3 copy-start
  555.0 60.5 %all-to-all-start.3 = ((bf16[96,32,384]{2,0,1:T(8,128)(2,1)}), bf16[96,32,384]{2,0,1:T(8,128)(2,1)S(1)}, u32[]{:S(2)}, u32[]{:S(2)}) async-start(bf16[96,32,384]{2,0,1:T(8,128)(2,1)} %copy.101), calls=%async_computation.3 | async-start | bytes 4718592 | tf_op jit(solution)/shard_map/all_to_all | solution.py:60
Sparse Core Ops, SparseCore 0:
  13.7 94.4 all-gather.4
  110.4 88.8 all-gather.6
  354.7 86.4 all-gather.8
